TPU v7x, 128 devices: a whole 4x4x4 slice. The times are simulated.
128 devices in a mesh: gx: 16 (over y, z_hi, core), gy: 8 (over z_lo, x).
Axes of the slice: x: 4, y: 4, z: 4 (z_hi: 2, z_lo: 2; z = z_hi * 2 + z_lo), core: 2. Of those that a mesh axis runs over, the one named last changes fastest.
Arguments:
- subspace: float32 [65536, 256], P(('gx', 'gy')), may hold values from -15 to 15
- diag_blocks: float32 [128, 512, 512], P(('gx', 'gy')), may hold values from -0.25 to 0.25
- onsite: float32 [65536], P(('gx', 'gy')), may hold values from 0.5 to 4
- coupling: float32 [2, 128, 12, 128, 128], P(None, ('gx', 'gy')), may hold values from -0.1875 to 0.1875
- tile_rows: int32 [2, 128, 12], P(None, ('gx', 'gy')), may hold values from 0 to 3
- tile_cols: int32 [2, 128, 12], P(None, ('gx', 'gy')), may hold values from 0 to 3
- partner: int32 [2, 128], replicated, may hold values from 0 to 127, as said below
Outputs:
- basis: float32 [65536, 256], P(('gx', 'gy'))
- gram_scaled: float32 [256, 256], replicated
Inputs may be any that keep to these rules, and one draw needn't show every extreme that they name: For each colour c there is one m_c, 1 to 127, with partner[c, i] = i XOR m_c for every device i; the two colours' m differ.
All inputs are finite; a program needn't handle non-finite values.
Results may differ from a plain program's by a relative error of at most 0.0003.
Values sent between devices are 32-bit elements; how exact they have to be, the bound alone decides.
No kernel may reach another device: no remote copies, remote signals or barrier semaphores. Data moves between devices by JAX's collectives and lax.ppermute only.
A program may use at most 64 MiB of HBM per device.

v0:
```python
import functools

import jax
import jax.numpy as jnp
from jax import lax
from jax.experimental import pallas as pl
from jax.experimental.pallas import tpu as pltpu
from jax.sharding import PartitionSpec as P

NS_ITERS = 12
AXES = ("gx", "gy")
VMEM = pl.BlockSpec(memory_space=pltpu.VMEM)
FAR = pl.BlockSpec(memory_space=pl.ANY)
SMEM = pl.BlockSpec(memory_space=pltpu.SMEM)
F32 = jnp.float32
BF16 = jnp.bfloat16
PAD = 16
VMEM_LIMIT = 28 << 20
NN = (((1,), (0,)), ((), ()))
TN = (((0,), (0,)), ((), ()))


def devices():
    return lax.axis_size("gx") * lax.axis_size("gy")


def swap(value, flip):
    return lax.ppermute(value, AXES, [(i, i ^ flip) for i in range(devices())])


def route(mask, core):
    above = lax.shift_right_logical(mask, jnp.int32(core.bit_length()))
    return (mask & (core - 1)) | (above * core), jnp.where((mask & core) != 0, 1, 0)


def exchange(place, flips_core, value):
    core = lax.axis_size("gy")
    keep = lambda kept: kept
    chips = [flip for flip in range(devices()) if not flip & core]
    movers = [functools.partial(swap, flip=flip) if flip else keep for flip in chips]
    value = lax.switch(place, movers, value)
    return lax.switch(flips_core, [keep, functools.partial(swap, flip=core)], value)


def split(value):
    high = value.astype(BF16)
    return high, (value - high.astype(F32)).astype(BF16)


def terms(high, low, right, dims=NN):
    dot = lambda a, b: lax.dot_general(a, b, dims, preferred_element_type=F32)
    return (dot(high, right[1]) + dot(low, right[0])) + dot(high, right[0])


def halves(size):
    return [pl.ds(start, size // 2) for start in (0, size // 2)]


def product(left, right, dims=NN):
    kept = 1 - dims[0][0][0]
    pieces = zip(*(jnp.split(part, 2, axis=kept) for part in left))
    return jnp.concatenate([terms(high, low, right, dims) for high, low in pieces], axis=0)


def indices(size):
    return tuple(lax.broadcasted_iota(jnp.int32, (size, size), axis) for axis in range(2))


def same_index(size):
    row, column = indices(size)
    return row == column


def prepare_kernel(
    core, tile_rows, tile_cols, partner, diag, onsite, own, tiles,
    high, low, acc, payload, place, flips_core, block,
):
    rows = own.shape[0]
    colours, count, size, _ = tiles.shape
    corners = range(rows // size)
    place[0], flips_core[0] = route(partner[0, 0], core)
    for c in range(colours):
        block[...] = jnp.zeros_like(block)
        for k in range(count):
            block[tile_rows[c, 0, k], tile_cols[c, 0, k]] += tiles[c, k]
        for r in corners:
            for s in corners:
                at = (pl.ds(r * size, size), pl.ds(s * size, size))
                high[(c, *at)], low[(c, *at)] = split(block[r, s])
    for r in corners:
        for s in corners:
            at = (pl.ds(r * size, size), pl.ds(s * size, size))
            value = diag[(0, *at)]
            if r == s:
                value += jnp.where(same_index(size), onsite[r : r + 1, :] - 2.0, 0.0)
            high[(colours, *at)], low[(colours, *at)] = split(value)
    value = own[...]
    parts = split(value)
    payload[pl.ds(0, rows), :] = value
    for half in halves(rows):
        acc[half, :] = terms(high[colours, half, :], low[colours, half, :], parts)
    for half in halves(rows):
        below = pl.ds(rows + half.start, half.size)
        payload[below, :] = terms(high[0, :, half], low[0, :, half], parts, TN)


def step_kernel(
    core, turn, partner, high, low, got, own, held_acc, held,
    acc, payload, place, flips_core, near_high, near_low, near, sems, near_sems,
):
    rows = own.shape[0]
    top, bottom = pl.ds(0, rows), pl.ds(rows, rows)
    colours = high.shape[0] - 1
    now = turn[0]
    colour, following = lax.rem(now, colours), lax.rem(now + 1, colours)
    last = colours * 2 - 1

    def fetch(index, slot):
        pairs = ((high, near_high), (low, near_low))
        return [
            pltpu.make_async_copy(far.at[index], close.at[slot], sems.at[slot, part])
            for part, (far, close) in enumerate(pairs)
        ]

    def wait(copies):
        for copy in copies:
            copy.wait()

    def below(half):
        return pl.ds(rows + half.start, half.size)

    def following_products(parts):
        for half in halves(rows):
            payload[below(half), :] = terms(near_high[0, :, half], near_low[0, :, half], parts, TN)

    backward, forward = fetch(following, 0), fetch(colour, 1)
    diagonal = fetch(colours, 2)
    arrived = [
        pltpu.make_async_copy(got.at[half], near.at[half], near_sems.at[part])
        for part, half in enumerate((top, bottom))
    ]
    for copy in backward + arrived[:1] + forward + arrived[1:]:
        copy.start()
    ends = colour == colours - 1

    @pl.when(now == colours - 1)
    def _():
        for copy in diagonal:
            copy.start()

    place[0], flips_core[0] = route(partner[following, 0], core)
    wait(backward)

    @pl.when(jnp.logical_not(ends))
    def _():
        value = held[top, :]
        payload[top, :] = value
        following_products(split(value))

    wait(arrived[:1] + forward + arrived[1:])
    mate = split(near[top, :])
    for half in halves(rows):
        kept = held_acc[half, :] + near[below(half), :]
        acc[half, :] = kept + terms(near_high[1, half, :], near_low[1, half, :], mate)

    @pl.when(now == colours - 1)
    def _():
        value = acc[...] * 0.25
        parts = split(value)
        payload[top, :] = value
        following_products(parts)
        wait(diagonal)
        for half in halves(rows):
            acc[half, :] = terms(near_high[2, half, :], near_low[2, half, :], parts)

    @pl.when(now == last)
    def _():
        payload[top, :] = acc[...] * 0.5 - own[...]


def gram_kernel(second_core, payload, keep, send, packed):
    states = payload.shape[1]
    half = states // 2
    parts = split(payload[pl.ds(0, payload.shape[0] // 2), :])
    gram = product(parts, parts, TN)
    row, column = indices(half)
    lower = gram[half:, half:]
    packed[pl.ds(0, half), :] = jnp.concatenate(
        [jnp.where(row <= column, gram[:half, :half], lower), gram[:half, half:]], axis=1
    )
    diagonal = jnp.sum(jnp.where(row == column, lower, 0.0), axis=0, keepdims=True)
    packed[pl.ds(half, PAD), :] = jnp.broadcast_to(
        jnp.concatenate([diagonal, diagonal], axis=1), (PAD, states)
    )
    share = packed.shape[0] // 2
    for own in range(2):

        @pl.when(second_core[0] == own)
        def _():
            keep[...] = packed[pl.ds(own * share, share), :]
            send[...] = packed[pl.ds((1 - own) * share, share), :]


def unpack_gram(second_core, value, other, packed):
    share = value.shape[0]
    for own in range(2):

        @pl.when(second_core[0] == own)
        def _():
            packed[pl.ds(own * share, share), :] = value[...]
            packed[pl.ds((1 - own) * share, share), :] = other[...]

    half = value.shape[1] // 2
    mixed, corner = packed[pl.ds(0, half), :half], packed[pl.ds(0, half), half:]
    turned = mixed.T
    row, column = indices(half)
    first = jnp.where(row <= column, mixed, turned)
    second = jnp.where(row > column, mixed, turned)
    second = jnp.where(row == column, packed[pl.ds(half, 1), :half], second)
    return jnp.concatenate(
        [jnp.concatenate([first, corner], axis=1), jnp.concatenate([corner.T, second], axis=1)],
        axis=0,
    )


def finish_kernel(order, second_core, value, other, payload, basis, scaled, packed):
    total_gram = unpack_gram(second_core, value, other, packed)
    scaled[...] = total_gram / order
    row, column = indices(total_gram.shape[0])
    eye = row == column
    on_diag = jnp.where(eye, total_gram, 0.0)
    total = jnp.sum(jnp.sum(on_diag, axis=0, keepdims=True), axis=1, keepdims=True)
    half = jnp.where(eye, 1.5, 0.0)
    iterate = total_gram / total
    inverse = half - 0.5 * iterate
    parts = split(inverse)
    iterate = product(split(iterate), parts)
    for turn in range(1, NS_ITERS):
        held = parts
        moved = split(iterate)
        parts = split(half - 0.5 * product(held, moved))
        if turn < NS_ITERS - 1:
            iterate = product(moved, parts)
        inverse = product(parts, held)
        parts = split(inverse)
    scale = lax.sqrt(jnp.full_like(total, order)) / lax.sqrt(total)
    rows = basis.shape[0]
    basis[...] = product(split(payload[pl.ds(0, rows), :]), parts) * scale


def call(kernel, outs, operands, scratch=(), scalars=0, far=0, routes=0, aliases=None, limit=VMEM_LIMIT):
    shapes = tuple(jax.ShapeDtypeStruct(shape, dtype) for shape, dtype in outs)
    shapes += (jax.ShapeDtypeStruct((1,), jnp.int32),) * routes
    return pl.pallas_call(
        kernel,
        out_shape=shapes,
        in_specs=[SMEM] * scalars + [FAR] * far + [VMEM] * (len(operands) - scalars - far),
        out_specs=(VMEM,) * len(outs) + (SMEM,) * routes,
        scratch_shapes=[pltpu.VMEM(s, F32) if isinstance(s, tuple) else s for s in scratch],
        input_output_aliases=aliases or {},
        compiler_params=pltpu.CompilerParams(vmem_limit_bytes=limit),
    )(*operands)


def sum_over_devices(keep, send):
    value = keep + swap(send, lax.axis_size("gy"))
    for flips in ((1, 3, 2), (4, 20, 16), (32, 96, 64)):
        others = [swap(value, flip) for flip in flips]
        value = (value + others[0]) + (others[1] + others[2])
    return value, swap(value, lax.axis_size("gy"))


def on_device(subspace, diag_blocks, onsite, coupling, tile_rows, tile_cols, partner):
    colours = partner.shape[0]
    rows, states = subspace.shape
    size = coupling.shape[3]
    blocks = rows // size
    core = lax.axis_size("gy")
    wide, double = ((rows, states), F32), ((2 * rows, states), F32)
    parts = ((colours + 1, rows, rows), BF16)
    high, low, *state = call(
        functools.partial(prepare_kernel, core),
        (parts, parts, wide, double),
        (
            tile_rows, tile_cols, partner,
            diag_blocks, onsite.reshape(blocks, size), subspace, coupling[:, 0],
        ),
        ((blocks, blocks, size, size),),
        scalars=3,
        routes=2,
        limit=None,
    )

    def step(turn, state):
        acc, payload, place, flips_core = state
        got = exchange(place[0], flips_core[0], payload)
        return call(
            functools.partial(step_kernel, core),
            (wide, double),
            (turn.reshape(1), partner, high, low, got, subspace, acc, payload),
            (
                *(pltpu.VMEM((3, rows, rows), BF16),) * 2,
                (2 * rows, states),
                pltpu.SemaphoreType.DMA((3, 2)),
                pltpu.SemaphoreType.DMA((2,)),
            ),
            scalars=2,
            far=3,
            routes=2,
            aliases={6: 0, 7: 1},
        )

    _, payload, _, _ = lax.fori_loop(0, 2 * colours, step, tuple(state))
    second_core = (lax.axis_index("gx") & 1).reshape(1)
    packed = (states // 2 + PAD, states)
    share = ((packed[0] // 2, states), F32)
    keep, send = call(gram_kernel, (share, share), (second_core, payload), (packed,), scalars=1)
    return call(
        functools.partial(finish_kernel, float(rows * devices())),
        (wide, ((states, states), F32)),
        (second_core, *sum_over_devices(keep, send), payload),
        (packed,),
        scalars=1,
    )


def solution(mesh):
    placed = (
        P(AXES, None),
        P(AXES, None, None),
        P(AXES),
        P(None, AXES, None, None, None),
        P(None, AXES, None),
        P(None, AXES, None),
        P(),
    )
    return jax.shard_map(
        on_device,
        mesh=mesh,
        in_specs=placed,
        out_specs=(P(AXES, None), P()),
        check_vma=False,
    )
```

profile of v0, /device:TPU:1, one launch (start us, length us, event | category | flops | bytes accessed | tf_op | source)
XLA Modules:
  0.0 194.5 jit_solution(59500436952655152)
XLA Ops:
  0.6 0.0 copy-start
  0.6 0.0 copy-start.1
  0.7 4.7 %shard_map.86 = (bf16[3,512,512]{2,1,0:T(8,128)(2,1)S(1)}, bf16[3,512,512]{2,1,0:T(8,128)(2,1)}, f32[512,256]{1,0:T(8,128)}, f32[1024,256]{1,0:T(8,128)S(1)}, s32[1]{0:T(128)}, /*index=5*/s32[1]{0:T(128)}) custom-call(s32[2,1,12]{2,1,0:T(1,128)} %tile_rows.1, s32[2,1,12]{2,1,0:T(1,128)} %tile_cols.1, s32[2,128]{1,0:T(2,128)} %partner.1, ...), custom_call_target="tpu_custom_call" | custom-call | tf_op jit(solution)/shard_map/pallas_call | solution.py:254
  5.3 0.0 copy-done
  5.3 0.0 copy-done.1
  5.3 150.9 %while.211 = (s32[]{:T(128)}, f32[512,256]{1,0:T(8,128)}, f32[1024,256]{1,0:T(8,128)S(1)}, s32[1]{0:T(128)}, s32[1]{0:T(128)}, /*index=5*/s32[2,128]{1,0:T(2,128...) while((s32[]{:T(128)}, f32[512,256]{1,0:T(8,128)}, ...), condition=%wide.region_67.0_spmd, body=%wide.region_0.0_spmd.sunk | while | flops 4 | bytes 10486013 | solution.py:313
  5.9 29.0 %conditional.4 = (f32[1024,256]{1,0:T(8,128)}) conditional(s32[]{:T(128)} %bitcast.11, f32[1024,256]{1,0:T(8,128)S(1)} %get-tuple-element.401.held, f32[1024,256]{1,0:T(8,128)S(1)} %get-tuple-element.401.held, f32[1024,256]{1,0:T(8,128)S(1)} %get-tuple-element.401.held, ...), branch_computations={%region_1.0_spmd, %region_2.0_spmd, %region_3.0_spmd, %region_4.0_... | conditional | bytes 4194352 | solution.py:41
  6.0 6.0 %collective-permute-start.21 = (f32[1024,256]{1,0:T(8,128)S(1)}, f32[1024,256]{1,0:T(8,128)}, u32[]{:S(2)}, u32[]{:S(2)}) collective-permute-start(f32[1024,256]{1,0:T(8,128)S(1)} %param.22), channel_id=1, source_target_pairs={{0,38},{1,39},{2,36},{3,37},{4,34},{5,35},{6,32},{7,33},{8,46},{9,... | collective-permute-start | bytes 3145736 | tf_op jit(solution)/shard_map/while/body/eval_jaxpr/cond/branch_22_fun/ppermute | solution.py:28
  12.0 23.0 %collective-permute-done.21 = f32[1024,256]{1,0:T(8,128)} collective-permute-done((f32[1024,256]{1,0:T(8,128)S(1)}, f32[1024,256]{1,0:T(8,128)}, u32[]{:S(2)}, u32[]{:S(2)}) %collective-permute-start.21) | collective-permute-done | bytes 1048608 | tf_op jit(solution)/shard_map/while/body/eval_jaxpr/cond/branch_22_fun/ppermute | solution.py:28
  35.6 4.3 %eval_jaxpr.5 = (f32[512,256]{1,0:T(8,128)}, f32[1024,256]{1,0:T(8,128)S(1)}, s32[1]{0:T(128)}, s32[1]{0:T(128)}) custom-call(s32[1]{0:T(128)} %bitcast.9.turn, s32[2,128]{1,0:T(2,128)S(1)} %get-tuple-element.417.partner, bf16[3,512,512]{2,1,0:T(8,128)(2,1)S(1)} %get-tuple-element.418.high, ...), custom_call_target="tpu_custom_call", output_to_operand_aliasing={{0}: (6, {}), {1}: (7, {})} | custom-call | tf_op jit(solution)/shard_map/while/body/eval_jaxpr/pallas_call | solution.py:254
  40.5 37.0 %conditional.4 = (f32[1024,256]{1,0:T(8,128)}) conditional(s32[]{:T(128)} %bitcast.11, f32[1024,256]{1,0:T(8,128)S(1)} %get-tuple-element.401.held, f32[1024,256]{1,0:T(8,128)S(1)} %get-tuple-element.401.held, f32[1024,256]{1,0:T(8,128)S(1)} %get-tuple-element.401.held, ...), branch_computations={%region_1.0_spmd, %region_2.0_spmd, %region_3.0_spmd, %region_4.0_... | conditional | bytes 4194352 | solution.py:41
  40.5 10.1 %collective-permute-start.48 = (f32[1024,256]{1,0:T(8,128)S(1)}, f32[1024,256]{1,0:T(8,128)}, u32[]{:S(2)}, u32[]{:S(2)}) collective-permute-start(f32[1024,256]{1,0:T(8,128)S(1)} %param.49), channel_id=1, source_target_pairs={{0,97},{1,96},{2,99},{3,98},{4,101},{5,100},{6,103},{7,102},{8,105... | collective-permute-start | bytes 3145736 | tf_op jit(solution)/shard_map/while/body/eval_jaxpr/cond/branch_49_fun/ppermute | solution.py:28
  50.6 26.8 %collective-permute-done.48 = f32[1024,256]{1,0:T(8,128)} collective-permute-done((f32[1024,256]{1,0:T(8,128)S(1)}, f32[1024,256]{1,0:T(8,128)}, u32[]{:S(2)}, u32[]{:S(2)}) %collective-permute-start.48) | collective-permute-done | bytes 1048608 | tf_op jit(solution)/shard_map/while/body/eval_jaxpr/cond/branch_49_fun/ppermute | solution.py:28
  78.1 5.3 %eval_jaxpr.5 = (f32[512,256]{1,0:T(8,128)}, f32[1024,256]{1,0:T(8,128)S(1)}, s32[1]{0:T(128)}, s32[1]{0:T(128)}) custom-call(s32[1]{0:T(128)} %bitcast.9.turn, s32[2,128]{1,0:T(2,128)S(1)} %get-tuple-element.417.partner, bf16[3,512,512]{2,1,0:T(8,128)(2,1)S(1)} %get-tuple-element.418.high, ...), custom_call_target="tpu_custom_call", output_to_operand_aliasing={{0}: (6, {}), {1}: (7, {})} | custom-call | tf_op jit(solution)/shard_map/while/body/eval_jaxpr/pallas_call | solution.py:254
  83.9 27.3 %conditional.4 = (f32[1024,256]{1,0:T(8,128)}) conditional(s32[]{:T(128)} %bitcast.11, f32[1024,256]{1,0:T(8,128)S(1)} %get-tuple-element.401.held, f32[1024,256]{1,0:T(8,128)S(1)} %get-tuple-element.401.held, f32[1024,256]{1,0:T(8,128)S(1)} %get-tuple-element.401.held, ...), branch_computations={%region_1.0_spmd, %region_2.0_spmd, %region_3.0_spmd, %region_4.0_... | conditional | bytes 4194352 | solution.py:41
  84.0 3.3 %collective-permute-start.21 = (f32[1024,256]{1,0:T(8,128)S(1)}, f32[1024,256]{1,0:T(8,128)}, u32[]{:S(2)}, u32[]{:S(2)}) collective-permute-start(f32[1024,256]{1,0:T(8,128)S(1)} %param.22), channel_id=1, source_target_pairs={{0,38},{1,39},{2,36},{3,37},{4,34},{5,35},{6,32},{7,33},{8,46},{9,... | collective-permute-start | bytes 3145736 | tf_op jit(solution)/shard_map/while/body/eval_jaxpr/cond/branch_22_fun/ppermute | solution.py:28
  87.3 23.9 %collective-permute-done.21 = f32[1024,256]{1,0:T(8,128)} collective-permute-done((f32[1024,256]{1,0:T(8,128)S(1)}, f32[1024,256]{1,0:T(8,128)}, u32[]{:S(2)}, u32[]{:S(2)}) %collective-permute-start.21) | collective-permute-done | bytes 1048608 | tf_op jit(solution)/shard_map/while/body/eval_jaxpr/cond/branch_22_fun/ppermute | solution.py:28
  111.9 4.3 %eval_jaxpr.5 = (f32[512,256]{1,0:T(8,128)}, f32[1024,256]{1,0:T(8,128)S(1)}, s32[1]{0:T(128)}, s32[1]{0:T(128)}) custom-call(s32[1]{0:T(128)} %bitcast.9.turn, s32[2,128]{1,0:T(2,128)S(1)} %get-tuple-element.417.partner, bf16[3,512,512]{2,1,0:T(8,128)(2,1)S(1)} %get-tuple-element.418.high, ...), custom_call_target="tpu_custom_call", output_to_operand_aliasing={{0}: (6, {}), {1}: (7, {})} | custom-call | tf_op jit(solution)/shard_map/while/body/eval_jaxpr/pallas_call | solution.py:254
  116.7 34.6 %conditional.4 = (f32[1024,256]{1,0:T(8,128)}) conditional(s32[]{:T(128)} %bitcast.11, f32[1024,256]{1,0:T(8,128)S(1)} %get-tuple-element.401.held, f32[1024,256]{1,0:T(8,128)S(1)} %get-tuple-element.401.held, f32[1024,256]{1,0:T(8,128)S(1)} %get-tuple-element.401.held, ...), branch_computations={%region_1.0_spmd, %region_2.0_spmd, %region_3.0_spmd, %region_4.0_... | conditional | bytes 4194352 | solution.py:41
  116.8 7.7 %collective-permute-start.48 = (f32[1024,256]{1,0:T(8,128)S(1)}, f32[1024,256]{1,0:T(8,128)}, u32[]{:S(2)}, u32[]{:S(2)}) collective-permute-start(f32[1024,256]{1,0:T(8,128)S(1)} %param.49), channel_id=1, source_target_pairs={{0,97},{1,96},{2,99},{3,98},{4,101},{5,100},{6,103},{7,102},{8,105... | collective-permute-start | bytes 3145736 | tf_op jit(solution)/shard_map/while/body/eval_jaxpr/cond/branch_49_fun/ppermute | solution.py:28
  124.5 26.8 %collective-permute-done.48 = f32[1024,256]{1,0:T(8,128)} collective-permute-done((f32[1024,256]{1,0:T(8,128)S(1)}, f32[1024,256]{1,0:T(8,128)}, u32[]{:S(2)}, u32[]{:S(2)}) %collective-permute-start.48) | collective-permute-done | bytes 1048608 | tf_op jit(solution)/shard_map/while/body/eval_jaxpr/cond/branch_49_fun/ppermute | solution.py:28
  151.9 4.1 %eval_jaxpr.5 = (f32[512,256]{1,0:T(8,128)}, f32[1024,256]{1,0:T(8,128)S(1)}, s32[1]{0:T(128)}, s32[1]{0:T(128)}) custom-call(s32[1]{0:T(128)} %bitcast.9.turn, s32[2,128]{1,0:T(2,128)S(1)} %get-tuple-element.417.partner, bf16[3,512,512]{2,1,0:T(8,128)(2,1)S(1)} %get-tuple-element.418.high, ...), custom_call_target="tpu_custom_call", output_to_operand_aliasing={{0}: (6, {}), {1}: (7, {})} | custom-call | tf_op jit(solution)/shard_map/while/body/eval_jaxpr/pallas_call | solution.py:254
  156.3 0.4 shard_map.87
  156.7 1.0 collective-permute-start.64
  157.7 0.9 collective-permute-done.64
  158.7 0.3 collective-permute-start.65
  159.0 2.4 %collective-permute-start.66 = (f32[72,256]{1,0:T(8,128)S(1)}, f32[72,256]{1,0:T(8,128)S(1)}, u32[]{:S(2)}, u32[]{:S(2)}) collective-permute-start(f32[72,256]{1,0:T(8,128)S(1)} %add.46), channel_id=1, source_target_pairs={{0,3},{1,2},{2,1},{3,0},{4,7},{5,6},{6,5},{7,4},{8,11},{9,10},{10,... | collective-permute-start | bytes 221192 | tf_op jit(solution)/shard_map/ppermute | solution.py:28
  161.5 0.5 collective-permute-start.67
  162.0 0.0 collective-permute-done.65
  162.0 1.4 collective-permute-done.66
  163.4 2.7 %collective-permute-done.67 = f32[72,256]{1,0:T(8,128)S(1)} collective-permute-done((f32[72,256]{1,0:T(8,128)S(1)}, f32[72,256]{1,0:T(8,128)S(1)}, u32[]{:S(2)}, u32[]{:S(2)}) %collective-permute-start.67) | collective-permute-done | bytes 73760 | tf_op jit(solution)/shard_map/ppermute | solution.py:28
  166.2 1.5 collective-permute-start.68
  167.7 2.1 %collective-permute-start.69 = (f32[72,256]{1,0:T(8,128)S(1)}, f32[72,256]{1,0:T(8,128)S(1)}, u32[]{:S(2)}, u32[]{:S(2)}) collective-permute-start(f32[72,256]{1,0:T(8,128)S(1)} %add_add_fusion.2), channel_id=1, source_target_pairs={{0,20},{1,21},{2,22},{3,23},{4,16},{5,17},{6,18},{7,19},{8,28},{9,... | collective-permute-start | bytes 221192 | tf_op jit(solution)/shard_map/ppermute | solution.py:28
  169.8 0.9 collective-permute-start.70
  170.7 0.0 collective-permute-done.68
  170.7 1.5 collective-permute-done.69
  172.1 2.7 %collective-permute-done.70 = f32[72,256]{1,0:T(8,128)S(1)} collective-permute-done((f32[72,256]{1,0:T(8,128)S(1)}, f32[72,256]{1,0:T(8,128)S(1)}, u32[]{:S(2)}, u32[]{:S(2)}) %collective-permute-start.70) | collective-permute-done | bytes 73760 | tf_op jit(solution)/shard_map/ppermute | solution.py:28
  174.9 0.1 collective-permute-start.71
  175.0 0.7 collective-permute-start.72
  175.7 2.5 %collective-permute-start.73 = (f32[72,256]{1,0:T(8,128)S(1)}, f32[72,256]{1,0:T(8,128)S(1)}, u32[]{:S(2)}, u32[]{:S(2)}) collective-permute-start(f32[72,256]{1,0:T(8,128)S(1)} %add_add_fusion.1), channel_id=1, source_target_pairs={{0,64},{1,65},{2,66},{3,67},{4,68},{5,69},{6,70},{7,71},{8,72},{9,... | collective-permute-start | bytes 221192 | tf_op jit(solution)/shard_map/ppermute | solution.py:28
  178.2 0.0 collective-permute-done.71
  178.2 1.2 collective-permute-done.72
  179.5 0.9 collective-permute-done.73
  180.4 5.2 %collective-permute-start.74 = (f32[72,256]{1,0:T(8,128)S(1)}, f32[72,256]{1,0:T(8,128)S(1)}, u32[]{:S(2)}, u32[]{:S(2)}) collective-permute-start(f32[72,256]{1,0:T(8,128)S(1)} %add_add_fusion.value), channel_id=1, source_target_pairs={{0,8},{1,9},{2,10},{3,11},{4,12},{5,13},{6,14},{7,15},{8,0},{9,1},... | collective-permute-start | bytes 221192 | tf_op jit(solution)/shard_map/ppermute | solution.py:28
  185.6 0.9 collective-permute-done.74.other
  186.5 8.0 %shard_map.88 = (f32[512,256]{1,0:T(8,128)}, f32[256,256]{1,0:T(8,128)}) custom-call(s32[1]{0:T(128)} %bitcast.3.second_core, f32[72,256]{1,0:T(8,128)S(1)} %add_add_fusion.value, f32[72,256]{1,0:T(8,128)S(1)} %collective-permute-done.74.other, f32[1024,256]{1,0:T(8,128)S(1)} %get-tuple-element.302.payload), custom_call_target="tpu_custom_call" | custom-call | tf_op jit(solution)/shard_map/pallas_call | solution.py:254
  (8 shorter events, 0.1 us)
Async XLA Ops:
  0.6 4.7 %copy-start = (f32[512,256]{1,0:T(8,128)S(1)}, f32[512,256]{1,0:T(8,128)}, u32[]{:S(2)}) copy-start(f32[512,256]{1,0:T(8,128)} %own.1) | copy-start | bytes 1572868
  0.6 4.7 %copy-start.1 = (s32[2,128]{1,0:T(2,128)S(1)}, s32[2,128]{1,0:T(2,128)}, u32[]{:S(2)}) copy-start(s32[2,128]{1,0:T(2,128)} %partner.1) | copy-start | bytes 3076
  6.0 29.0 %collective-permute-start.21 = (f32[1024,256]{1,0:T(8,128)S(1)}, f32[1024,256]{1,0:T(8,128)}, u32[]{:S(2)}, u32[]{:S(2)}) collective-permute-start(f32[1024,256]{1,0:T(8,128)S(1)} %param.22), channel_id=1, source_target_pairs={{0,38},{1,39},{2,36},{3,37},{4,34},{5,35},{6,32},{7,33},{8,46},{9,... | collective-permute-start | bytes 3145736 | tf_op jit(solution)/shard_map/while/body/eval_jaxpr/cond/branch_22_fun/ppermute | solution.py:28
  40.5 36.9 %collective-permute-start.48 = (f32[1024,256]{1,0:T(8,128)S(1)}, f32[1024,256]{1,0:T(8,128)}, u32[]{:S(2)}, u32[]{:S(2)}) collective-permute-start(f32[1024,256]{1,0:T(8,128)S(1)} %param.49), channel_id=1, source_target_pairs={{0,97},{1,96},{2,99},{3,98},{4,101},{5,100},{6,103},{7,102},{8,105... | collective-permute-start | bytes 3145736 | tf_op jit(solution)/shard_map/while/body/eval_jaxpr/cond/branch_49_fun/ppermute | solution.py:28
  84.0 27.2 %collective-permute-start.21 = (f32[1024,256]{1,0:T(8,128)S(1)}, f32[1024,256]{1,0:T(8,128)}, u32[]{:S(2)}, u32[]{:S(2)}) collective-permute-start(f32[1024,256]{1,0:T(8,128)S(1)} %param.22), channel_id=1, source_target_pairs={{0,38},{1,39},{2,36},{3,37},{4,34},{5,35},{6,32},{7,33},{8,46},{9,... | collective-permute-start | bytes 3145736 | tf_op jit(solution)/shard_map/while/body/eval_jaxpr/cond/branch_22_fun/ppermute | solution.py:28
  116.8 34.5 %collective-permute-start.48 = (f32[1024,256]{1,0:T(8,128)S(1)}, f32[1024,256]{1,0:T(8,128)}, u32[]{:S(2)}, u32[]{:S(2)}) collective-permute-start(f32[1024,256]{1,0:T(8,128)S(1)} %param.49), channel_id=1, source_target_pairs={{0,97},{1,96},{2,99},{3,98},{4,101},{5,100},{6,103},{7,102},{8,105... | collective-permute-start | bytes 3145736 | tf_op jit(solution)/shard_map/while/body/eval_jaxpr/cond/branch_49_fun/ppermute | solution.py:28
  156.7 2.0 %collective-permute-start.64 = (f32[72,256]{1,0:T(8,128)S(1)}, f32[72,256]{1,0:T(8,128)S(1)}, u32[]{:S(2)}, u32[]{:S(2)}) collective-permute-start(f32[72,256]{1,0:T(8,128)S(1)} %get-tuple-element.304), channel_id=1, source_target_pairs={{0,8},{1,9},{2,10},{3,11},{4,12},{5,13},{6,14},{7,15},{8,0},{9,1},... | collective-permute-start | bytes 221192 | tf_op jit(solution)/shard_map/ppermute | solution.py:28
  158.7 3.3 %collective-permute-start.65 = (f32[72,256]{1,0:T(8,128)S(1)}, f32[72,256]{1,0:T(8,128)S(1)}, u32[]{:S(2)}, u32[]{:S(2)}) collective-permute-start(f32[72,256]{1,0:T(8,128)S(1)} %add.46), channel_id=1, source_target_pairs={{0,1},{1,0},{2,3},{3,2},{4,5},{5,4},{6,7},{7,6},{8,9},{9,8},{10,11... | collective-permute-start | bytes 221192 | tf_op jit(solution)/shard_map/ppermute | solution.py:28
  159.0 4.4 %collective-permute-start.66 = (f32[72,256]{1,0:T(8,128)S(1)}, f32[72,256]{1,0:T(8,128)S(1)}, u32[]{:S(2)}, u32[]{:S(2)}) collective-permute-start(f32[72,256]{1,0:T(8,128)S(1)} %add.46), channel_id=1, source_target_pairs={{0,3},{1,2},{2,1},{3,0},{4,7},{5,6},{6,5},{7,4},{8,11},{9,10},{10,... | collective-permute-start | bytes 221192 | tf_op jit(solution)/shard_map/ppermute | solution.py:28
  161.5 4.7 %collective-permute-start.67 = (f32[72,256]{1,0:T(8,128)S(1)}, f32[72,256]{1,0:T(8,128)S(1)}, u32[]{:S(2)}, u32[]{:S(2)}) collective-permute-start(f32[72,256]{1,0:T(8,128)S(1)} %add.46), channel_id=1, source_target_pairs={{0,2},{1,3},{2,0},{3,1},{4,6},{5,7},{6,4},{7,5},{8,10},{9,11},{10,... | collective-permute-start | bytes 221192 | tf_op jit(solution)/shard_map/ppermute | solution.py:28
  166.2 4.5 %collective-permute-start.68 = (f32[72,256]{1,0:T(8,128)S(1)}, f32[72,256]{1,0:T(8,128)S(1)}, u32[]{:S(2)}, u32[]{:S(2)}) collective-permute-start(f32[72,256]{1,0:T(8,128)S(1)} %add_add_fusion.2), channel_id=1, source_target_pairs={{0,4},{1,5},{2,6},{3,7},{4,0},{5,1},{6,2},{7,3},{8,12},{9,13},{10,... | collective-permute-start | bytes 221192 | tf_op jit(solution)/shard_map/ppermute | solution.py:28
  167.7 4.4 %collective-permute-start.69 = (f32[72,256]{1,0:T(8,128)S(1)}, f32[72,256]{1,0:T(8,128)S(1)}, u32[]{:S(2)}, u32[]{:S(2)}) collective-permute-start(f32[72,256]{1,0:T(8,128)S(1)} %add_add_fusion.2), channel_id=1, source_target_pairs={{0,20},{1,21},{2,22},{3,23},{4,16},{5,17},{6,18},{7,19},{8,28},{9,... | collective-permute-start | bytes 221192 | tf_op jit(solution)/shard_map/ppermute | solution.py:28
  169.8 5.1 %collective-permute-start.70 = (f32[72,256]{1,0:T(8,128)S(1)}, f32[72,256]{1,0:T(8,128)S(1)}, u32[]{:S(2)}, u32[]{:S(2)}) collective-permute-start(f32[72,256]{1,0:T(8,128)S(1)} %add_add_fusion.2), channel_id=1, source_target_pairs={{0,16},{1,17},{2,18},{3,19},{4,20},{5,21},{6,22},{7,23},{8,24},{9,... | collective-permute-start | bytes 221192 | tf_op jit(solution)/shard_map/ppermute | solution.py:28
  174.9 3.3 %collective-permute-start.71 = (f32[72,256]{1,0:T(8,128)S(1)}, f32[72,256]{1,0:T(8,128)S(1)}, u32[]{:S(2)}, u32[]{:S(2)}) collective-permute-start(f32[72,256]{1,0:T(8,128)S(1)} %add_add_fusion.1), channel_id=1, source_target_pairs={{0,32},{1,33},{2,34},{3,35},{4,36},{5,37},{6,38},{7,39},{8,40},{9,... | collective-permute-start | bytes 221192 | tf_op jit(solution)/shard_map/ppermute | solution.py:28
  175.0 4.5 %collective-permute-start.72 = (f32[72,256]{1,0:T(8,128)S(1)}, f32[72,256]{1,0:T(8,128)S(1)}, u32[]{:S(2)}, u32[]{:S(2)}) collective-permute-start(f32[72,256]{1,0:T(8,128)S(1)} %add_add_fusion.1), channel_id=1, source_target_pairs={{0,96},{1,97},{2,98},{3,99},{4,100},{5,101},{6,102},{7,103},{8,104... | collective-permute-start | bytes 221192 | tf_op jit(solution)/shard_map/ppermute | solution.py:28
  175.7 4.7 %collective-permute-start.73 = (f32[72,256]{1,0:T(8,128)S(1)}, f32[72,256]{1,0:T(8,128)S(1)}, u32[]{:S(2)}, u32[]{:S(2)}) collective-permute-start(f32[72,256]{1,0:T(8,128)S(1)} %add_add_fusion.1), channel_id=1, source_target_pairs={{0,64},{1,65},{2,66},{3,67},{4,68},{5,69},{6,70},{7,71},{8,72},{9,... | collective-permute-start | bytes 221192 | tf_op jit(solution)/shard_map/ppermute | solution.py:28
  180.4 6.1 %collective-permute-start.74 = (f32[72,256]{1,0:T(8,128)S(1)}, f32[72,256]{1,0:T(8,128)S(1)}, u32[]{:S(2)}, u32[]{:S(2)}) collective-permute-start(f32[72,256]{1,0:T(8,128)S(1)} %add_add_fusion.value), channel_id=1, source_target_pairs={{0,8},{1,9},{2,10},{3,11},{4,12},{5,13},{6,14},{7,15},{8,0},{9,1},... | collective-permute-start | bytes 221192 | tf_op jit(solution)/shard_map/ppermute | solution.py:28
where the time goes:
time: 191 us; the launch traced here: 194 us
  waiting for transfers between devices  113 us (59%)
  starting transfers between devices  44.5 us (23%)
  Pallas kernels  31 us (16%)
  loops' own time  5.31 us (3%)
    ppermute x15, waiting for transfers between devices, swap(): return lax.ppermute(value, AXES, [(i, i ^ flip) for i in range(devices())])  113 us
    ppermute x15, starting transfers between devices, swap(): return lax.ppermute(value, AXES, [(i, i ^ flip) for i in range(devices())])  44.5 us
    pallas_call x7, Pallas kernels, call(): pl.pallas_call(kernel, out_shape=shapes, in_specs=[SMEM] * scalars + [FAR...  31 us
    another operation x1, loops' own time, on_device(): _, payload, _, _ = lax.fori_loop(0, 2 * colours, step, tuple(state))  5.04 us
  transfers between devices with their start and end apart: 15, of which 12 were waited for; matrix products, arithmetic and copies ran while one was open for 0% of the time, Pallas kernels for 0%

commit v1 on v0

--- a/solution.py
+++ b/solution.py
@@ -72,25 +72,33 @@
 
 
 def prepare_kernel(
-    core, tile_rows, tile_cols, partner, diag, onsite, own, tiles,
-    high, low, acc, payload, place, flips_core, block,
+    core, tile_rows, tile_cols, partner, far_diag, far_own, far_tiles, onsite,
+    high, low, acc, payload, place, flips_core, block, diag, own, tiles, sems,
 ):
     rows = own.shape[0]
     colours, count, size, _ = tiles.shape
+    pairs = [(far_tiles.at[c], tiles.at[c]) for c in range(colours)]
+    pairs += [(far_own, own), (far_diag.at[0], diag)]
+    loads = [pltpu.make_async_copy(*pair, sems.at[i]) for i, pair in enumerate(pairs)]
+    for load in loads:
+        load.start()
     corners = range(rows // size)
     place[0], flips_core[0] = route(partner[0, 0], core)
     for c in range(colours):
         block[...] = jnp.zeros_like(block)
+        loads[c].wait()
         for k in range(count):
             block[tile_rows[c, 0, k], tile_cols[c, 0, k]] += tiles[c, k]
         for r in corners:
             for s in corners:
                 at = (pl.ds(r * size, size), pl.ds(s * size, size))
                 high[(c, *at)], low[(c, *at)] = split(block[r, s])
+    loads[colours].wait()
+    loads[colours + 1].wait()
     for r in corners:
         for s in corners:
             at = (pl.ds(r * size, size), pl.ds(s * size, size))
-            value = diag[(0, *at)]
+            value = diag[at]
             if r == s:
                 value += jnp.where(same_index(size), onsite[r : r + 1, :] - 2.0, 0.0)
             high[(colours, *at)], low[(colours, *at)] = split(value)
@@ -283,10 +291,17 @@
         (parts, parts, wide, double),
         (
             tile_rows, tile_cols, partner,
-            diag_blocks, onsite.reshape(blocks, size), subspace, coupling[:, 0],
+            diag_blocks, subspace, coupling[:, 0], onsite.reshape(blocks, size),
         ),
-        ((blocks, blocks, size, size),),
+        (
+            (blocks, blocks, size, size),
+            (rows, rows),
+            (rows, states),
+            (colours, *coupling.shape[2:]),
+            pltpu.SemaphoreType.DMA((colours + 2,)),
+        ),
         scalars=3,
+        far=3,
         routes=2,
         limit=None,
     )

time: 191 us -> 195 us (1.021); the launches traced: 194 us -> 193 us
  starting transfers between devices: 44.5 us -> 35.3 us
  waiting for transfers between devices: 113 us -> 121 us
    ppermute x15, starting transfers between devices: 44.5 us -> 35.3 us  [swap(): return lax.ppermute(value, AXES, [(i, i ^ flip) for i in range(devices())])]
    ppermute x15, waiting for transfers between devices: 113 us -> 121 us  [swap(): return lax.ppermute(value, AXES, [(i, i ^ flip) for i in range(devices())])]
  transfers between devices with their start and end apart: 15 -> 15, of which waited for: 12 -> 11; matrix products, arithmetic and copies ran while one was open for 0% -> 0% of each run, Pallas kernels for 0% -> 0%
where the time goes in v1:
time: 195 us; the launch traced here: 193 us
  waiting for transfers between devices  121 us (62%)
  starting transfers between devices  35.3 us (18%)
  Pallas kernels  30.7 us (16%)
  loops' own time  5.32 us (3%)
    ppermute x15, waiting for transfers between devices, swap(): return lax.ppermute(value, AXES, [(i, i ^ flip) for i in range(devices())])  121 us
    ppermute x15, starting transfers between devices, swap(): return lax.ppermute(value, AXES, [(i, i ^ flip) for i in range(devices())])  35.3 us
    pallas_call x7, Pallas kernels, call(): pl.pallas_call(kernel, out_shape=shapes, in_specs=[SMEM] * scalars + [FAR...  30.7 us
    another operation x1, loops' own time, on_device(): _, payload, _, _ = lax.fori_loop(0, 2 * colours, step, tuple(state))  5.04 us
  transfers between devices with their start and end apart: 15, of which 11 were waited for; matrix products, arithmetic and copies ran while one was open for 0% of the time, Pallas kernels for 0%

profile of v1, /device:TPU:1, one launch (start us, length us, event | category | flops | bytes accessed | tf_op | source)
XLA Modules:
  0.0 192.9 jit_solution(13041224894062745782)
XLA Ops:
  0.6 0.0 copy-start
  0.6 0.0 copy-start.1
  0.7 4.4 %shard_map.86 = (bf16[3,512,512]{2,1,0:T(8,128)(2,1)S(1)}, bf16[3,512,512]{2,1,0:T(8,128)(2,1)}, f32[512,256]{1,0:T(8,128)}, f32[1024,256]{1,0:T(8,128)S(1)}, s32[1]{0:T(128)}, /*index=5*/s32[1]{0:T(128)}) custom-call(s32[2,1,12]{2,1,0:T(1,128)} %tile_rows.1, s32[2,1,12]{2,1,0:T(1,128)} %tile_cols.1, s32[2,128]{1,0:T(2,128)} %partner.1, ...), custom_call_target="tpu_custom_call" | custom-call | tf_op jit(solution)/shard_map/pallas_call | solution.py:262
  5.0 0.0 copy-done
  5.0 0.0 copy-done.1
  5.0 153.9 %while.211 = (s32[]{:T(128)}, f32[512,256]{1,0:T(8,128)}, f32[1024,256]{1,0:T(8,128)S(1)}, s32[1]{0:T(128)}, s32[1]{0:T(128)}, /*index=5*/s32[2,128]{1,0:T(2,128...) while((s32[]{:T(128)}, f32[512,256]{1,0:T(8,128)}, ...), condition=%wide.region_67.0_spmd, body=%wide.region_0.0_spmd.sunk | while | flops 4 | bytes 10486013 | solution.py:328
  5.6 28.5 %conditional.4 = (f32[1024,256]{1,0:T(8,128)}) conditional(s32[]{:T(128)} %bitcast.11, f32[1024,256]{1,0:T(8,128)S(1)} %get-tuple-element.401.held, f32[1024,256]{1,0:T(8,128)S(1)} %get-tuple-element.401.held, f32[1024,256]{1,0:T(8,128)S(1)} %get-tuple-element.401.held, ...), branch_computations={%region_1.0_spmd, %region_2.0_spmd, %region_3.0_spmd, %region_4.0_... | conditional | bytes 4194352 | solution.py:41
  5.7 5.5 %collective-permute-start.23 = (f32[1024,256]{1,0:T(8,128)S(1)}, f32[1024,256]{1,0:T(8,128)}, u32[]{:S(2)}, u32[]{:S(2)}) collective-permute-start(f32[1024,256]{1,0:T(8,128)S(1)} %param.24), channel_id=1, source_target_pairs={{0,48},{1,49},{2,50},{3,51},{4,52},{5,53},{6,54},{7,55},{8,56},{9,... | collective-permute-start | bytes 3145736 | tf_op jit(solution)/shard_map/while/body/eval_jaxpr/cond/branch_24_fun/ppermute | solution.py:28
  11.2 23.0 %collective-permute-done.23 = f32[1024,256]{1,0:T(8,128)} collective-permute-done((f32[1024,256]{1,0:T(8,128)S(1)}, f32[1024,256]{1,0:T(8,128)}, u32[]{:S(2)}, u32[]{:S(2)}) %collective-permute-start.23) | collective-permute-done | bytes 1048608 | tf_op jit(solution)/shard_map/while/body/eval_jaxpr/cond/branch_24_fun/ppermute | solution.py:28
  34.8 4.3 %eval_jaxpr.5 = (f32[512,256]{1,0:T(8,128)}, f32[1024,256]{1,0:T(8,128)S(1)}, s32[1]{0:T(128)}, s32[1]{0:T(128)}) custom-call(s32[1]{0:T(128)} %bitcast.9.turn, s32[2,128]{1,0:T(2,128)S(1)} %get-tuple-element.417.partner, bf16[3,512,512]{2,1,0:T(8,128)(2,1)S(1)} %get-tuple-element.418.high, ...), custom_call_target="tpu_custom_call", output_to_operand_aliasing={{0}: (6, {}), {1}: (7, {})} | custom-call | tf_op jit(solution)/shard_map/while/body/eval_jaxpr/pallas_call | solution.py:262
  39.6 41.0 %conditional.4 = (f32[1024,256]{1,0:T(8,128)}) conditional(s32[]{:T(128)} %bitcast.11, f32[1024,256]{1,0:T(8,128)S(1)} %get-tuple-element.401.held, f32[1024,256]{1,0:T(8,128)S(1)} %get-tuple-element.401.held, f32[1024,256]{1,0:T(8,128)S(1)} %get-tuple-element.401.held, ...), branch_computations={%region_1.0_spmd, %region_2.0_spmd, %region_3.0_spmd, %region_4.0_... | conditional | bytes 4194352 | solution.py:41
  39.7 9.7 %collective-permute-start.57 = (f32[1024,256]{1,0:T(8,128)S(1)}, f32[1024,256]{1,0:T(8,128)}, u32[]{:S(2)}, u32[]{:S(2)}) collective-permute-start(f32[1024,256]{1,0:T(8,128)S(1)} %param.58), channel_id=1, source_target_pairs={{0,114},{1,115},{2,112},{3,113},{4,118},{5,119},{6,116},{7,117},{8... | collective-permute-start | bytes 3145736 | tf_op jit(solution)/shard_map/while/body/eval_jaxpr/cond/branch_58_fun/ppermute | solution.py:28
  49.4 31.3 %collective-permute-done.57 = f32[1024,256]{1,0:T(8,128)} collective-permute-done((f32[1024,256]{1,0:T(8,128)S(1)}, f32[1024,256]{1,0:T(8,128)}, u32[]{:S(2)}, u32[]{:S(2)}) %collective-permute-start.57) | collective-permute-done | bytes 1048608 | tf_op jit(solution)/shard_map/while/body/eval_jaxpr/cond/branch_58_fun/ppermute | solution.py:28
  81.3 5.3 %eval_jaxpr.5 = (f32[512,256]{1,0:T(8,128)}, f32[1024,256]{1,0:T(8,128)S(1)}, s32[1]{0:T(128)}, s32[1]{0:T(128)}) custom-call(s32[1]{0:T(128)} %bitcast.9.turn, s32[2,128]{1,0:T(2,128)S(1)} %get-tuple-element.417.partner, bf16[3,512,512]{2,1,0:T(8,128)(2,1)S(1)} %get-tuple-element.418.high, ...), custom_call_target="tpu_custom_call", output_to_operand_aliasing={{0}: (6, {}), {1}: (7, {})} | custom-call | tf_op jit(solution)/shard_map/while/body/eval_jaxpr/pallas_call | solution.py:262
  87.2 26.4 %conditional.4 = (f32[1024,256]{1,0:T(8,128)}) conditional(s32[]{:T(128)} %bitcast.11, f32[1024,256]{1,0:T(8,128)S(1)} %get-tuple-element.401.held, f32[1024,256]{1,0:T(8,128)S(1)} %get-tuple-element.401.held, f32[1024,256]{1,0:T(8,128)S(1)} %get-tuple-element.401.held, ...), branch_computations={%region_1.0_spmd, %region_2.0_spmd, %region_3.0_spmd, %region_4.0_... | conditional | bytes 4194352 | solution.py:41
  87.2 0.1 collective-permute-start.23
  87.3 26.2 %collective-permute-done.23 = f32[1024,256]{1,0:T(8,128)} collective-permute-done((f32[1024,256]{1,0:T(8,128)S(1)}, f32[1024,256]{1,0:T(8,128)}, u32[]{:S(2)}, u32[]{:S(2)}) %collective-permute-start.23) | collective-permute-done | bytes 1048608 | tf_op jit(solution)/shard_map/while/body/eval_jaxpr/cond/branch_24_fun/ppermute | solution.py:28
  114.2 4.3 %eval_jaxpr.5 = (f32[512,256]{1,0:T(8,128)}, f32[1024,256]{1,0:T(8,128)S(1)}, s32[1]{0:T(128)}, s32[1]{0:T(128)}) custom-call(s32[1]{0:T(128)} %bitcast.9.turn, s32[2,128]{1,0:T(2,128)S(1)} %get-tuple-element.417.partner, bf16[3,512,512]{2,1,0:T(8,128)(2,1)S(1)} %get-tuple-element.418.high, ...), custom_call_target="tpu_custom_call", output_to_operand_aliasing={{0}: (6, {}), {1}: (7, {})} | custom-call | tf_op jit(solution)/shard_map/while/body/eval_jaxpr/pallas_call | solution.py:262
  119.1 34.9 %conditional.4 = (f32[1024,256]{1,0:T(8,128)}) conditional(s32[]{:T(128)} %bitcast.11, f32[1024,256]{1,0:T(8,128)S(1)} %get-tuple-element.401.held, f32[1024,256]{1,0:T(8,128)S(1)} %get-tuple-element.401.held, f32[1024,256]{1,0:T(8,128)S(1)} %get-tuple-element.401.held, ...), branch_computations={%region_1.0_spmd, %region_2.0_spmd, %region_3.0_spmd, %region_4.0_... | conditional | bytes 4194352 | solution.py:41
  119.2 3.5 %collective-permute-start.57 = (f32[1024,256]{1,0:T(8,128)S(1)}, f32[1024,256]{1,0:T(8,128)}, u32[]{:S(2)}, u32[]{:S(2)}) collective-permute-start(f32[1024,256]{1,0:T(8,128)S(1)} %param.58), channel_id=1, source_target_pairs={{0,114},{1,115},{2,112},{3,113},{4,118},{5,119},{6,116},{7,117},{8... | collective-permute-start | bytes 3145736 | tf_op jit(solution)/shard_map/while/body/eval_jaxpr/cond/branch_58_fun/ppermute | solution.py:28
  122.7 31.3 %collective-permute-done.57 = f32[1024,256]{1,0:T(8,128)} collective-permute-done((f32[1024,256]{1,0:T(8,128)S(1)}, f32[1024,256]{1,0:T(8,128)}, u32[]{:S(2)}, u32[]{:S(2)}) %collective-permute-start.57) | collective-permute-done | bytes 1048608 | tf_op jit(solution)/shard_map/while/body/eval_jaxpr/cond/branch_58_fun/ppermute | solution.py:28
  154.6 4.1 %eval_jaxpr.5 = (f32[512,256]{1,0:T(8,128)}, f32[1024,256]{1,0:T(8,128)S(1)}, s32[1]{0:T(128)}, s32[1]{0:T(128)}) custom-call(s32[1]{0:T(128)} %bitcast.9.turn, s32[2,128]{1,0:T(2,128)S(1)} %get-tuple-element.417.partner, bf16[3,512,512]{2,1,0:T(8,128)(2,1)S(1)} %get-tuple-element.418.high, ...), custom_call_target="tpu_custom_call", output_to_operand_aliasing={{0}: (6, {}), {1}: (7, {})} | custom-call | tf_op jit(solution)/shard_map/while/body/eval_jaxpr/pallas_call | solution.py:262
  158.9 0.4 shard_map.87
  159.4 1.0 collective-permute-start.64
  160.4 0.9 collective-permute-done.64
  161.3 0.4 collective-permute-start.65
  161.7 0.7 collective-permute-start.66
  162.4 2.3 %collective-permute-start.67 = (f32[72,256]{1,0:T(8,128)S(1)}, f32[72,256]{1,0:T(8,128)S(1)}, u32[]{:S(2)}, u32[]{:S(2)}) collective-permute-start(f32[72,256]{1,0:T(8,128)S(1)} %add.46), channel_id=1, source_target_pairs={{0,2},{1,3},{2,0},{3,1},{4,6},{5,7},{6,4},{7,5},{8,10},{9,11},{10,... | collective-permute-start | bytes 221192 | tf_op jit(solution)/shard_map/ppermute | solution.py:28
  164.7 0.0 collective-permute-done.65
  164.7 1.5 collective-permute-done.66
  166.1 1.0 collective-permute-done.67
  167.2 0.6 collective-permute-start.68
  167.8 0.2 collective-permute-start.69
  168.0 2.5 %collective-permute-start.70 = (f32[72,256]{1,0:T(8,128)S(1)}, f32[72,256]{1,0:T(8,128)S(1)}, u32[]{:S(2)}, u32[]{:S(2)}) collective-permute-start(f32[72,256]{1,0:T(8,128)S(1)} %add_add_fusion.2), channel_id=1, source_target_pairs={{0,16},{1,17},{2,18},{3,19},{4,20},{5,21},{6,22},{7,23},{8,24},{9,... | collective-permute-start | bytes 221192 | tf_op jit(solution)/shard_map/ppermute | solution.py:28
  170.5 0.0 collective-permute-done.68
  170.5 2.5 %collective-permute-done.69 = f32[72,256]{1,0:T(8,128)S(1)} collective-permute-done((f32[72,256]{1,0:T(8,128)S(1)}, f32[72,256]{1,0:T(8,128)S(1)}, u32[]{:S(2)}, u32[]{:S(2)}) %collective-permute-start.69) | collective-permute-done | bytes 73760 | tf_op jit(solution)/shard_map/ppermute | solution.py:28
  173.0 0.0 collective-permute-done.70
  173.0 0.1 collective-permute-start.71
  173.1 0.7 collective-permute-start.72
  173.8 2.5 %collective-permute-start.73 = (f32[72,256]{1,0:T(8,128)S(1)}, f32[72,256]{1,0:T(8,128)S(1)}, u32[]{:S(2)}, u32[]{:S(2)}) collective-permute-start(f32[72,256]{1,0:T(8,128)S(1)} %add_add_fusion.1), channel_id=1, source_target_pairs={{0,64},{1,65},{2,66},{3,67},{4,68},{5,69},{6,70},{7,71},{8,72},{9,... | collective-permute-start | bytes 221192 | tf_op jit(solution)/shard_map/ppermute | solution.py:28
  176.4 0.0 collective-permute-done.71
  176.4 1.2 collective-permute-done.72
  177.6 0.9 collective-permute-done.73
  178.6 5.4 %collective-permute-start.74 = (f32[72,256]{1,0:T(8,128)S(1)}, f32[72,256]{1,0:T(8,128)S(1)}, u32[]{:S(2)}, u32[]{:S(2)}) collective-permute-start(f32[72,256]{1,0:T(8,128)S(1)} %add_add_fusion.value), channel_id=1, source_target_pairs={{0,8},{1,9},{2,10},{3,11},{4,12},{5,13},{6,14},{7,15},{8,0},{9,1},... | collective-permute-start | bytes 221192 | tf_op jit(solution)/shard_map/ppermute | solution.py:28
  184.0 0.9 collective-permute-done.74.other
  184.9 8.0 %shard_map.88 = (f32[512,256]{1,0:T(8,128)}, f32[256,256]{1,0:T(8,128)}) custom-call(s32[1]{0:T(128)} %bitcast.3.second_core, f32[72,256]{1,0:T(8,128)S(1)} %add_add_fusion.value, f32[72,256]{1,0:T(8,128)S(1)} %collective-permute-done.74.other, f32[1024,256]{1,0:T(8,128)S(1)} %get-tuple-element.302.payload), custom_call_target="tpu_custom_call" | custom-call | tf_op jit(solution)/shard_map/pallas_call | solution.py:262
  (8 shorter events, 0.1 us)
Async XLA Ops:
  0.6 4.4 %copy-start = (f32[512,256]{1,0:T(8,128)S(1)}, f32[512,256]{1,0:T(8,128)}, u32[]{:S(2)}) copy-start(f32[512,256]{1,0:T(8,128)} %far_own.1) | copy-start | bytes 1572868
  0.6 4.4 %copy-start.1 = (s32[2,128]{1,0:T(2,128)S(1)}, s32[2,128]{1,0:T(2,128)}, u32[]{:S(2)}) copy-start(s32[2,128]{1,0:T(2,128)} %partner.1) | copy-start | bytes 3076
  5.7 28.5 %collective-permute-start.23 = (f32[1024,256]{1,0:T(8,128)S(1)}, f32[1024,256]{1,0:T(8,128)}, u32[]{:S(2)}, u32[]{:S(2)}) collective-permute-start(f32[1024,256]{1,0:T(8,128)S(1)} %param.24), channel_id=1, source_target_pairs={{0,48},{1,49},{2,50},{3,51},{4,52},{5,53},{6,54},{7,55},{8,56},{9,... | collective-permute-start | bytes 3145736 | tf_op jit(solution)/shard_map/while/body/eval_jaxpr/cond/branch_24_fun/ppermute | solution.py:28
  39.7 41.0 %collective-permute-start.57 = (f32[1024,256]{1,0:T(8,128)S(1)}, f32[1024,256]{1,0:T(8,128)}, u32[]{:S(2)}, u32[]{:S(2)}) collective-permute-start(f32[1024,256]{1,0:T(8,128)S(1)} %param.58), channel_id=1, source_target_pairs={{0,114},{1,115},{2,112},{3,113},{4,118},{5,119},{6,116},{7,117},{8... | collective-permute-start | bytes 3145736 | tf_op jit(solution)/shard_map/while/body/eval_jaxpr/cond/branch_58_fun/ppermute | solution.py:28
  87.2 26.3 %collective-permute-start.23 = (f32[1024,256]{1,0:T(8,128)S(1)}, f32[1024,256]{1,0:T(8,128)}, u32[]{:S(2)}, u32[]{:S(2)}) collective-permute-start(f32[1024,256]{1,0:T(8,128)S(1)} %param.24), channel_id=1, source_target_pairs={{0,48},{1,49},{2,50},{3,51},{4,52},{5,53},{6,54},{7,55},{8,56},{9,... | collective-permute-start | bytes 3145736 | tf_op jit(solution)/shard_map/while/body/eval_jaxpr/cond/branch_24_fun/ppermute | solution.py:28
  119.2 34.8 %collective-permute-start.57 = (f32[1024,256]{1,0:T(8,128)S(1)}, f32[1024,256]{1,0:T(8,128)}, u32[]{:S(2)}, u32[]{:S(2)}) collective-permute-start(f32[1024,256]{1,0:T(8,128)S(1)} %param.58), channel_id=1, source_target_pairs={{0,114},{1,115},{2,112},{3,113},{4,118},{5,119},{6,116},{7,117},{8... | collective-permute-start | bytes 3145736 | tf_op jit(solution)/shard_map/while/body/eval_jaxpr/cond/branch_58_fun/ppermute | solution.py:28
  159.4 2.0 %collective-permute-start.64 = (f32[72,256]{1,0:T(8,128)S(1)}, f32[72,256]{1,0:T(8,128)S(1)}, u32[]{:S(2)}, u32[]{:S(2)}) collective-permute-start(f32[72,256]{1,0:T(8,128)S(1)} %get-tuple-element.304), channel_id=1, source_target_pairs={{0,8},{1,9},{2,10},{3,11},{4,12},{5,13},{6,14},{7,15},{8,0},{9,1},... | collective-permute-start | bytes 221192 | tf_op jit(solution)/shard_map/ppermute | solution.py:28
  161.3 3.3 %collective-permute-start.65 = (f32[72,256]{1,0:T(8,128)S(1)}, f32[72,256]{1,0:T(8,128)S(1)}, u32[]{:S(2)}, u32[]{:S(2)}) collective-permute-start(f32[72,256]{1,0:T(8,128)S(1)} %add.46), channel_id=1, source_target_pairs={{0,1},{1,0},{2,3},{3,2},{4,5},{5,4},{6,7},{7,6},{8,9},{9,8},{10,11... | collective-permute-start | bytes 221192 | tf_op jit(solution)/shard_map/ppermute | solution.py:28
  161.7 4.4 %collective-permute-start.66 = (f32[72,256]{1,0:T(8,128)S(1)}, f32[72,256]{1,0:T(8,128)S(1)}, u32[]{:S(2)}, u32[]{:S(2)}) collective-permute-start(f32[72,256]{1,0:T(8,128)S(1)} %add.46), channel_id=1, source_target_pairs={{0,3},{1,2},{2,1},{3,0},{4,7},{5,6},{6,5},{7,4},{8,11},{9,10},{10,... | collective-permute-start | bytes 221192 | tf_op jit(solution)/shard_map/ppermute | solution.py:28
  162.4 4.8 %collective-permute-start.67 = (f32[72,256]{1,0:T(8,128)S(1)}, f32[72,256]{1,0:T(8,128)S(1)}, u32[]{:S(2)}, u32[]{:S(2)}) collective-permute-start(f32[72,256]{1,0:T(8,128)S(1)} %add.46), channel_id=1, source_target_pairs={{0,2},{1,3},{2,0},{3,1},{4,6},{5,7},{6,4},{7,5},{8,10},{9,11},{10,... | collective-permute-start | bytes 221192 | tf_op jit(solution)/shard_map/ppermute | solution.py:28
  167.2 3.3 %collective-permute-start.68 = (f32[72,256]{1,0:T(8,128)S(1)}, f32[72,256]{1,0:T(8,128)S(1)}, u32[]{:S(2)}, u32[]{:S(2)}) collective-permute-start(f32[72,256]{1,0:T(8,128)S(1)} %add_add_fusion.2), channel_id=1, source_target_pairs={{0,4},{1,5},{2,6},{3,7},{4,0},{5,1},{6,2},{7,3},{8,12},{9,13},{10,... | collective-permute-start | bytes 221192 | tf_op jit(solution)/shard_map/ppermute | solution.py:28
  167.8 5.2 %collective-permute-start.69 = (f32[72,256]{1,0:T(8,128)S(1)}, f32[72,256]{1,0:T(8,128)S(1)}, u32[]{:S(2)}, u32[]{:S(2)}) collective-permute-start(f32[72,256]{1,0:T(8,128)S(1)} %add_add_fusion.2), channel_id=1, source_target_pairs={{0,20},{1,21},{2,22},{3,23},{4,16},{5,17},{6,18},{7,19},{8,28},{9,... | collective-permute-start | bytes 221192 | tf_op jit(solution)/shard_map/ppermute | solution.py:28
  168.0 5.0 %collective-permute-start.70 = (f32[72,256]{1,0:T(8,128)S(1)}, f32[72,256]{1,0:T(8,128)S(1)}, u32[]{:S(2)}, u32[]{:S(2)}) collective-permute-start(f32[72,256]{1,0:T(8,128)S(1)} %add_add_fusion.2), channel_id=1, source_target_pairs={{0,16},{1,17},{2,18},{3,19},{4,20},{5,21},{6,22},{7,23},{8,24},{9,... | collective-permute-start | bytes 221192 | tf_op jit(solution)/shard_map/ppermute | solution.py:28
  173.0 3.3 %collective-permute-start.71 = (f32[72,256]{1,0:T(8,128)S(1)}, f32[72,256]{1,0:T(8,128)S(1)}, u32[]{:S(2)}, u32[]{:S(2)}) collective-permute-start(f32[72,256]{1,0:T(8,128)S(1)} %add_add_fusion.1), channel_id=1, source_target_pairs={{0,32},{1,33},{2,34},{3,35},{4,36},{5,37},{6,38},{7,39},{8,40},{9,... | collective-permute-start | bytes 221192 | tf_op jit(solution)/shard_map/ppermute | solution.py:28
  173.1 4.5 %collective-permute-start.72 = (f32[72,256]{1,0:T(8,128)S(1)}, f32[72,256]{1,0:T(8,128)S(1)}, u32[]{:S(2)}, u32[]{:S(2)}) collective-permute-start(f32[72,256]{1,0:T(8,128)S(1)} %add_add_fusion.1), channel_id=1, source_target_pairs={{0,96},{1,97},{2,98},{3,99},{4,100},{5,101},{6,102},{7,103},{8,104... | collective-permute-start | bytes 221192 | tf_op jit(solution)/shard_map/ppermute | solution.py:28
  173.8 4.7 %collective-permute-start.73 = (f32[72,256]{1,0:T(8,128)S(1)}, f32[72,256]{1,0:T(8,128)S(1)}, u32[]{:S(2)}, u32[]{:S(2)}) collective-permute-start(f32[72,256]{1,0:T(8,128)S(1)} %add_add_fusion.1), channel_id=1, source_target_pairs={{0,64},{1,65},{2,66},{3,67},{4,68},{5,69},{6,70},{7,71},{8,72},{9,... | collective-permute-start | bytes 221192 | tf_op jit(solution)/shard_map/ppermute | solution.py:28
  178.6 6.3 %collective-permute-start.74 = (f32[72,256]{1,0:T(8,128)S(1)}, f32[72,256]{1,0:T(8,128)S(1)}, u32[]{:S(2)}, u32[]{:S(2)}) collective-permute-start(f32[72,256]{1,0:T(8,128)S(1)} %add_add_fusion.value), channel_id=1, source_target_pairs={{0,8},{1,9},{2,10},{3,11},{4,12},{5,13},{6,14},{7,15},{8,0},{9,1},... | collective-permute-start | bytes 221192 | tf_op jit(solution)/shard_map/ppermute | solution.py:28
